TPU v7x, 32 devices: a whole 2x2x4 slice. The times are simulated.
32 devices in a mesh: ep: 8 (over y, x, core), tp: 4 (over z).
Axes of the slice: x: 2, y: 2, z: 4, core: 2. Of those that a mesh axis runs over, the one named last changes fastest.
Arguments:
- tokens: bfloat16 [256, 4096], P('ep', 'tp'), may hold values from -6 to 6
- norm_gains: float32 [2, 4096], replicated, may hold values from 0.1 to 1.9
- router: bfloat16 [2, 4096, 16], replicated, as said below
- w_gate: bfloat16 [2, 16, 4096, 768], P(None, 'ep', None, 'tp'), may hold values from -0.09375 to 0.09375
- w_up: bfloat16 [2, 16, 4096, 768], P(None, 'ep', None, 'tp'), may hold values from -0.09375 to 0.09375
- w_down: bfloat16 [2, 16, 768, 4096], P(None, 'ep', 'tp'), may hold values from -0.21875 to 0.21875
- expert_ids: int32 [2, 256, 8], P(None, 'ep'), may hold values from 0 to 15, all different within a row; in each aligned block of 32 rows (0 to 31, 32 to 63, ...) at most 32 rows name the same one
Outputs:
- hidden_out: bfloat16 [256, 4096], P('ep', 'tp')
Inputs may be any that keep to these rules, and one draw needn't show every extreme that they name: `expert_ids`: each entry names an expert of 0 to 15; the 8 entries of a token differ; among the 32 tokens of one ep index in one layer no expert is named more than 32 times, and in some such blocks one is named exactly 32 times. `router`: entries of order 2 / sqrt(4096); all columns of a layer may share a common added vector with entries of order 50 / sqrt(4096).
All inputs are finite; a program needn't handle non-finite values.
Results may differ from a plain program's by a relative error of at most 0.02.
Values may be sent and summed in bfloat16 or wider, within the bound.
A program may use at most 64 MiB of HBM per device.

v0:
```python
import jax
import jax.numpy as jnp
from jax import lax
from jax.sharding import PartitionSpec as P

TOP = 8
LAYERS = 2
norm_eps = 1e-06


def body(tokens, norm_gains, router, w_gate, w_up, w_down, expert_ids):
    n_tp = lax.axis_size("tp")
    n_ep = lax.axis_size("ep")
    local_width = tokens.shape[1]
    full_width = local_width * n_tp
    rows_dev = tokens.shape[0]
    local_exp = w_gate.shape[1]
    experts = local_exp * n_ep
    capacity = 2 * rows_dev * TOP // experts
    current = tokens
    for layer_idx in range(LAYERS):
        gain = norm_gains[layer_idx]
        weight = router[layer_idx]
        ids = expert_ids[layer_idx]
        normed = None
        whole = lax.all_gather(current, "tp", axis=1, tiled=True)
        wide_rows = whole.astype(jnp.float32)
        square_sum = jnp.sum(wide_rows * wide_rows, axis=1)
        scaled = (wide_rows * gain[None, :]).astype(jnp.bfloat16)
        raw_logits = jnp.dot(scaled, weight, preferred_element_type=jnp.float32)
        inverse = lax.rsqrt(square_sum / full_width + norm_eps)
        normed = (scaled.astype(jnp.float32) * inverse[:, None]).astype(jnp.bfloat16)
        logits = raw_logits * inverse[:, None]
        choose = ids[:, :, None] == lax.iota(jnp.int32, experts)[None, None, :]
        picked = jnp.sum(jnp.where(choose, logits[:, None, :], 0.0), axis=-1)
        gate_probs = jax.nn.softmax(picked, axis=-1)
        onehot = choose.reshape(rows_dev * TOP, experts).astype(jnp.int32)
        earlier = jnp.cumsum(onehot, axis=0) - onehot
        slot_index = jnp.sum(earlier * onehot, axis=1).reshape(rows_dev, TOP)
        slot_key = ids * capacity + slot_index
        slot_hits = slot_key[None, :, :] == lax.iota(jnp.int32, experts * capacity)[:, None, None]
        route_matrix = jnp.any(slot_hits, axis=-1).astype(jnp.bfloat16)
        combine_matrix = jnp.sum(jnp.where(slot_hits, gate_probs[None, :, :], 0.0), axis=-1).T
        outgoing = jnp.dot(route_matrix, normed, preferred_element_type=jnp.float32).astype(
            jnp.bfloat16
        )
        outgoing = outgoing.reshape(n_ep, local_exp * capacity, full_width)
        incoming = lax.all_to_all(outgoing, "ep", split_axis=0, concat_axis=0, tiled=True)
        arrived = incoming.reshape(n_ep, local_exp, capacity, full_width).transpose(1, 0, 2, 3)
        arrived = arrived.reshape(local_exp, n_ep * capacity, full_width)
        gate_proj = jnp.einsum(
            "erd,edf->erf", arrived, w_gate[layer_idx], preferred_element_type=jnp.float32
        )
        up_proj = jnp.einsum(
            "erd,edf->erf", arrived, w_up[layer_idx], preferred_element_type=jnp.float32
        )
        inner = (jax.nn.silu(gate_proj) * up_proj).astype(jnp.bfloat16)
        down_local = w_down[layer_idx]

        def project():
            down_piece = lax.slice_in_dim(down_local, 0, local_width * lax.axis_size("tp"), axis=2)
            return jnp.einsum("erf,efd->der", inner, down_piece, preferred_element_type=jnp.float32)

        summed = lax.psum_scatter(
            project().astype(jnp.bfloat16), "tp", scatter_dimension=0, tiled=True
        ).astype(jnp.float32)
        out_rows = summed.astype(jnp.bfloat16).reshape(local_width, local_exp, n_ep, capacity)
        out_rows = out_rows.transpose(2, 1, 3, 0).reshape(n_ep, local_exp * capacity, local_width)
        returned = lax.all_to_all(out_rows, "ep", split_axis=0, concat_axis=0, tiled=True)
        returned = returned.reshape(experts * capacity, local_width).astype(jnp.float32)
        moe_out = jnp.dot(combine_matrix, returned, precision=lax.Precision.HIGHEST)
        current = (current.astype(jnp.float32) + moe_out).astype(jnp.bfloat16)
    return current


def solution(mesh):
    in_specs = (
        P("ep", "tp"),
        P(),
        P(),
        P(None, "ep", None, "tp"),
        P(None, "ep", None, "tp"),
        P(None, "ep", "tp", None),
        P(None, "ep", None),
    )
    out_specs = P("ep", "tp")
    return jax.shard_map(body, mesh=mesh, in_specs=in_specs, out_specs=out_specs, check_vma=False)
```

profile of v0, /device:TPU:0, one launch (start us, length us, event | category | flops | bytes accessed | tf_op | source)
XLA Modules:
  0.0 376.2 jit_solution(15348728780867839647)
XLA Ops:
  6.5 0.7 fusion.79
  7.3 0.1 eq.102
  7.4 0.1 eq.98
  7.5 0.6 reduce-window.14
  8.1 0.2 slice_reduce_fusion.1
  8.3 0.1 fusion.69
  8.4 0.1 reshape.147
  8.5 0.2 fusion.41
  8.8 0.9 fusion.78
  9.6 15.9 %all_gather.6 = bf16[32,4096]{1,0:T(8,128)(2,1)S(1)} all-gather(bf16[32,1024]{1,0:T(8,128)(2,1)} %param.7), channel_id=1, replica_groups=mesh['ep'=8,'tp'=4] {'tp'}, dimensions={1}, use_global_device_ids=true | all-gather | bytes 327680 | tf_op jit(solution)/shard_map/all_gather | solution.py:26
  25.5 0.2 fusion.37
  25.7 1.3 convolution_convert_fusion.3
  27.0 52.8 %all_to_all.20 = bf16[8,64,4096]{2,1,0:T(8,128)(2,1)S(1)} all-to-all(bf16[8,64,4096]{2,1,0:T(8,128)(2,1)S(1)} %bitcast.120), channel_id=1, replica_groups=mesh['ep'=8,'tp'=4] {'ep'}, dimensions={0} | all-to-all | bytes 8388608 | tf_op jit(solution)/shard_map/all_to_all | solution.py:48
  79.8 0.5 copy.30
  80.3 2.0 copy-done
  82.3 1.5 fusion.10
  83.9 8.8 %fusion = bf16[4096,2,256]{0,2,1:T(8,128)(2,1)} fusion(bf16[2,2,192,4096]{3,2,1,0:T(8,128)(2,1)} %param.12, bf16[2,256,4096]{2,1,0:T(8,128)(2,1)} %bitcast.125, bf16[2,2,4096,192]{2,3,1,0:T(8,128)(2,1)} %param.11, f32[2,256,192]{1,2,0:T(8,128)S(1)} %fusion.10), kind=kOutput, calls=%fused_computation.4 | convolution fusion | flops 1613299712 | bytes 15073280 | tf_op jit(solution)/shard_map/erf,efd->der/dot_general | solution.py:62
  92.8 0.1 eq.118
  92.8 0.1 eq.114
  92.9 0.6 reduce-window.16
  93.5 0.2 slice_reduce_fusion
  93.8 0.1 fusion.66
  93.9 0.1 reshape.155
  94.0 0.2 convolution_multiply_fusion.1
  94.1 75.1 %reduce-scatter.3.cloned.1.call-done = bf16[1024,2,256]{0,2,1:T(8,128)(2,1)} async-done(((bf16[4096,2,256]{0,2,1:T(8,128)(2,1)}), bf16[1024,2,256]{0,2,1:T(8,128)(2,1)}) %reduce-scatter.3.cloned.1.call-update) | async-done | bytes 1048592 | tf_op jit(solution)/shard_map/reduce_scatter | solution.py:64
  169.3 2.3 copy.31
  171.6 3.6 all-to-all-start.1
  175.4 0.1 copy.29
  175.4 0.2 fusion.40
  175.7 0.2 select_reduce_fusion.1
  175.9 14.7 %all-to-all-done.1 = bf16[8,64,1024]{2,1,0:T(8,128)(2,1)S(1)} async-done(((bf16[8,64,1024]{2,1,0:T(8,128)(2,1)}), bf16[8,64,1024]{2,1,0:T(8,128)(2,1)S(1)}, u32[]{:S(2)}, u32[]{:S(2)}) %all-to-all-start.1) | async-done | bytes 1048608 | tf_op jit(solution)/shard_map/all_to_all | solution.py:69
  190.6 0.6 fusion.30
  191.2 14.4 %all_gather.7 = bf16[32,4096]{1,0:T(8,128)(2,1)S(1)} all-gather(bf16[32,1024]{1,0:T(8,128)(2,1)S(1)} %fusion.30), channel_id=1, replica_groups=mesh['ep'=8,'tp'=4] {'tp'}, dimensions={1}, use_global_device_ids=true | all-gather | bytes 327680 | tf_op jit(solution)/shard_map/all_gather | solution.py:26
  205.6 0.2 fusion.39
  205.8 1.3 convolution_convert_fusion.1
  207.1 51.8 %all_to_all.21 = bf16[8,64,4096]{2,1,0:T(8,128)(2,1)S(1)} all-to-all(bf16[8,64,4096]{2,1,0:T(8,128)(2,1)S(1)} %bitcast.122), channel_id=1, replica_groups=mesh['ep'=8,'tp'=4] {'ep'}, dimensions={0} | all-to-all | bytes 8388608 | tf_op jit(solution)/shard_map/all_to_all | solution.py:48
  258.9 0.5 copy.36
  259.4 2.0 copy-done.1
  261.4 1.5 fusion.5
  262.9 8.8 %fusion.1 = bf16[4096,2,256]{0,2,1:T(8,128)(2,1)} fusion(bf16[2,2,192,4096]{3,2,1,0:T(8,128)(2,1)} %param.12, bf16[2,256,4096]{2,1,0:T(8,128)(2,1)} %bitcast.127, bf16[2,2,4096,192]{2,3,1,0:T(8,128)(2,1)} %param.11, f32[2,256,192]{1,2,0:T(8,128)S(1)} %fusion.5), kind=kOutput, calls=%fused_computation.5 | convolution fusion | flops 1613299712 | bytes 15073280 | tf_op jit(solution)/shard_map/erf,efd->der/dot_general | solution.py:62
  271.7 75.0 %reduce-scatter.5.cloned.1.call-done = bf16[1024,2,256]{0,2,1:T(8,128)(2,1)} async-done(((bf16[4096,2,256]{0,2,1:T(8,128)(2,1)}), bf16[1024,2,256]{0,2,1:T(8,128)(2,1)}) %reduce-scatter.5.cloned.1.call-update) | async-done | bytes 1048592 | tf_op jit(solution)/shard_map/reduce_scatter | solution.py:64
  346.7 2.3 copy.37
  349.0 3.7 all-to-all-start.3
  352.7 0.2 convolution_multiply_fusion
  353.0 0.1 copy.35
  353.1 0.2 select_reduce_fusion
  353.3 14.8 %all-to-all-done.3 = bf16[8,64,1024]{2,1,0:T(8,128)(2,1)S(1)} async-done(((bf16[8,64,1024]{2,1,0:T(8,128)(2,1)}), bf16[8,64,1024]{2,1,0:T(8,128)(2,1)S(1)}, u32[]{:S(2)}, u32[]{:S(2)}) %all-to-all-start.3) | async-done | bytes 1048608 | tf_op jit(solution)/shard_map/all_to_all | solution.py:69
  368.1 1.2 fusion.31
  (40 shorter events, 0.6 us)
Async XLA Ops:
  6.5 162.8 %reduce-scatter.3.cloned.1.call-start = ((), (), s32[]{:S(2)}) async-start(), calls=%async_computation.6 | async-start | bytes 5242880 | tf_op jit(solution)/shard_map/reduce_scatter | solution.py:64
  27.0 55.3 %slice-start = ((s8[6291456]{0:T(1024)(128)(4,1)}), s8[4194304]{0:T(1024)(128)(4,1)S(1)}, s32[]{:S(2)}) async-start(s8[6291456]{0:T(1024)(128)(4,1)} %bitcast.136), calls=%async_computation.8 | async-start | bytes 8388608
  79.8 2.5 slice-start.1
  80.3 2.0 copy-start
  92.6 1.3 copy-start.3
  92.6 98.0 %copy-start.2 = (bf16[32,1024]{1,0:T(8,128)(2,1)S(1)}, bf16[32,1024]{1,0:T(8,128)(2,1)}, u32[]{:S(2)}) copy-start(bf16[32,1024]{1,0:T(8,128)(2,1)} %param.7) | copy-start | bytes 196612
  171.6 19.0 %all-to-all-start.1 = ((bf16[8,64,1024]{2,1,0:T(8,128)(2,1)}), bf16[8,64,1024]{2,1,0:T(8,128)(2,1)S(1)}, u32[]{:S(2)}, u32[]{:S(2)}) async-start(bf16[8,64,1024]{2,1,0:T(8,128)(2,1)} %bitcast.16), calls=%async_computation.2 | async-start | bytes 2097152 | tf_op jit(solution)/shard_map/all_to_all | solution.py:69
  175.2 171.5 %reduce-scatter.5.cloned.1.call-start = ((), (), s32[]{:S(2)}) async-start(), calls=%async_computation.7 | async-start | bytes 5242880 | tf_op jit(solution)/shard_map/reduce_scatter | solution.py:64
  207.1 54.3 %slice-start.2 = ((s8[6291456]{0:T(1024)(128)(4,1)}), s8[4194304]{0:T(1024)(128)(4,1)S(1)}, s32[]{:S(2)}) async-start(s8[6291456]{0:T(1024)(128)(4,1)} %bitcast.138), calls=%async_computation.10 | async-start | bytes 8388608
  258.9 2.5 slice-start.3
  259.4 2.0 copy-start.1
  349.0 19.0 %all-to-all-start.3 = ((bf16[8,64,1024]{2,1,0:T(8,128)(2,1)}), bf16[8,64,1024]{2,1,0:T(8,128)(2,1)S(1)}, u32[]{:S(2)}, u32[]{:S(2)}) async-start(bf16[8,64,1024]{2,1,0:T(8,128)(2,1)} %bitcast.34), calls=%async_computation.5 | async-start | bytes 2097152 | tf_op jit(solution)/shard_map/all_to_all | solution.py:69
Sparse Core Ops, SparseCore 0:
  92.8 76.4 reduce-scatter.2
  271.8 74.8 reduce-scatter.4
where the time goes:
time: 377 us; the launch traced here: 376 us
  waiting for transfers between devices  180 us (48%)
  blocking collectives  135 us (36%)
  matrix products  25.5 us (7%)
  between operations  13.6 us (4%)
  local copies, waits for them, and re-layouts  12.3 us (3%)
  starting transfers between devices  7.32 us (2%)
    reduce_scatter x2, waiting for transfers between devices, body(): lax.psum_scatter(project().astype(jnp.bfloat16), 'tp', scatter_dimension=...  150 us
    all_to_all x2, blocking collectives, body(): lax.all_to_all(outgoing, 'ep', split_axis=0, concat_axis=0, tiled=True)  105 us
    all_gather x2, blocking collectives, body(): whole = lax.all_gather(current, 'tp', axis=1, tiled=True)  30.2 us
    all_to_all x2, waiting for transfers between devices, body(): lax.all_to_all(out_rows, 'ep', split_axis=0, concat_axis=0, tiled=True)  29.5 us
    dot_general x2, matrix products, project(): jnp.einsum('erf,efd->der', inner, down_piece, preferred_element_type=jnp....  17.6 us
  transfers between devices with their start and end apart: 4, of which 4 were waited for; matrix products, arithmetic and copies ran while one was open for 1% of the time, Pallas kernels for 0%

commit v1 on v0

--- a/solution.py
+++ b/solution.py
@@ -2,10 +2,23 @@
 import jax.numpy as jnp
 from jax import lax
 from jax.sharding import PartitionSpec as P
+from jax.lax import axis_index, ppermute, psum
 
 TOP = 8
 LAYERS = 2
 norm_eps = 1e-06
+
+
+def _check_map(x_in, join_dim, inner_x):
+    state_now, far_arr = (x_in.shape[:join_dim], x_in.shape[join_dim + 1 :])
+    local_next = x_in.reshape(*state_now, inner_x, -1, *far_arr)
+    return jnp.moveaxis(local_next, join_dim, 0)
+
+
+def limits_name(x_part, array_axis):
+    x_part = jnp.moveaxis(x_part, 0, array_axis)
+    z = x_part.shape
+    return x_part.reshape(*z[:array_axis], z[array_axis] * z[array_axis + 1], *z[array_axis + 2 :])
 
 
 def body(tokens, norm_gains, router, w_gate, w_up, w_down, expert_ids):
@@ -45,7 +58,28 @@
             jnp.bfloat16
         )
         outgoing = outgoing.reshape(n_ep, local_exp * capacity, full_width)
-        incoming = lax.all_to_all(outgoing, "ep", split_axis=0, concat_axis=0, tiled=True)
+
+        def refer_kinds_on(point, w_in, mesh_dim, in_array):
+            y_new = psum(1, mesh_dim)
+            outer = axis_index(mesh_dim)
+            current_block, b_now = (y_new, outer)
+            parts_out = _check_map(point, in_array, current_block)
+            column = [parts_out[b_now]]
+            q = 1
+            while q < current_block:
+                item_now = parts_out[b_now ^ q]
+                column.append(
+                    ppermute(
+                        item_now,
+                        mesh_dim,
+                        [(hop_no, hop_no ^ q) for hop_no in range(current_block)],
+                    )
+                )
+                q += 1
+            parts_out = jnp.stack(column, axis=0)[b_now ^ jnp.arange(current_block)]
+            return limits_name(parts_out, w_in)
+
+        incoming = refer_kinds_on(outgoing, 0, "ep", 0)
         arrived = incoming.reshape(n_ep, local_exp, capacity, full_width).transpose(1, 0, 2, 3)
         arrived = arrived.reshape(local_exp, n_ep * capacity, full_width)
         gate_proj = jnp.einsum(

time: 377 us -> 406 us (1.077)
  blocking collectives: 135 us -> 30.4 us
  waiting for transfers between devices: 180 us -> 269 us
  local copies, waits for them, and re-layouts: 12.3 us -> 41.1 us
  starting transfers between devices: 7.32 us -> 19 us
    all_to_all x2 -> x0, blocking collectives: 105 us -> none  [body(): lax.all_to_all(outgoing, 'ep', split_axis=0, concat_axis=0, tiled=True)]
    ppermute x0 -> x14, waiting for transfers between devices: none -> 88 us  [refer_kinds_on(): ppermute(item_now, mesh_dim, [(hop_no, hop_no ^ q) for hop_no in range(cu...]
    ppermute x0 -> x14, starting transfers between devices: none -> 11.7 us  [refer_kinds_on(): ppermute(item_now, mesh_dim, [(hop_no, hop_no ^ q) for hop_no in range(cu...]
    unnamed x18 -> x22, local copies, waits for them, and re-layouts: 4.13 us -> 14.2 us
    gather x0 -> x2, local copies, waits for them, and re-layouts: none -> 9.94 us  [refer_kinds_on(): parts_out = jnp.stack(column, axis=0)[b_now ^ jnp.arange(current_block)]]
    another operation x3 -> x7, local copies, waits for them, and re-layouts: 0.19 us -> 7.24 us  [the longest x2 5.34 us: body(): incoming.reshape(n_ep, local_exp, capacity, full_width)]
  transfers between devices with their start and end apart: 4 -> 18, of which waited for: 4 -> 8; matrix products, arithmetic and copies ran while one was open for 1% -> 3% of each run, Pallas kernels for 0% -> 0%
where the time goes in v1:
time: 406 us; the launch traced here: 405 us
  waiting for transfers between devices  269 us (66%)
  local copies, waits for them, and re-layouts  41.1 us (10%)
  blocking collectives  30.4 us (7%)
  matrix products  29.3 us (7%)
  starting transfers between devices  19 us (5%)
  between operations  13.6 us (3%)
    reduce_scatter x2, waiting for transfers between devices, body(): lax.psum_scatter(project().astype(jnp.bfloat16), 'tp', scatter_dimension=...  151 us
    ppermute x14, waiting for transfers between devices, refer_kinds_on(): ppermute(item_now, mesh_dim, [(hop_no, hop_no ^ q) for hop_no in range(cu...  88 us
    all_gather x2, blocking collectives, body(): whole = lax.all_gather(current, 'tp', axis=1, tiled=True)  30.4 us
    all_to_all x2, waiting for transfers between devices, body(): lax.all_to_all(out_rows, 'ep', split_axis=0, concat_axis=0, tiled=True)  29.5 us
    dot_general x2, matrix products, project(): jnp.einsum('erf,efd->der', inner, down_piece, preferred_element_type=jnp....  17.6 us
    unnamed x22, local copies, waits for them, and re-layouts  14.2 us
    ppermute x14, starting transfers between devices, refer_kinds_on(): ppermute(item_now, mesh_dim, [(hop_no, hop_no ^ q) for hop_no in range(cu...  11.7 us
    gather x2, local copies, waits for them, and re-layouts, refer_kinds_on(): parts_out = jnp.stack(column, axis=0)[b_now ^ jnp.arange(current_block)]  9.94 us
  transfers between devices with their start and end apart: 18, of which 8 were waited for; matrix products, arithmetic and copies ran while one was open for 3% of the time, Pallas kernels for 0%

profile of v1, /device:TPU:0, one launch (start us, length us, event | category | flops | bytes accessed | tf_op | source)
XLA Modules:
  0.0 405.2 jit_solution(17291219655644058048)
XLA Ops:
  8.8 0.9 fusion.79
  9.6 15.9 %all_gather.6 = bf16[32,4096]{1,0:T(8,128)(2,1)S(1)} all-gather(bf16[32,1024]{1,0:T(8,128)(2,1)} %param.7), channel_id=1, replica_groups=mesh['ep'=8,'tp'=4] {'tp'}, dimensions={1}, use_global_device_ids=true | all-gather | bytes 327680 | tf_op jit(solution)/shard_map/all_gather | solution.py:39
  25.7 1.3 convolution_convert_fusion.3
  27.0 1.3 dynamic-slice_bitcast_fusion.7
  28.3 2.6 collective-permute-start.6
  31.4 0.8 collective-permute-start.4
  32.9 1.6 collective-permute-start.1
  34.5 0.8 bitcast_dynamic-update-slice_fusion.13
  35.3 30.7 %collective-permute-done.1 = bf16[1,64,4096]{2,1,0:T(8,128)(2,1)S(1)} collective-permute-done((bf16[1,64,4096]{2,1,0:T(8,128)(2,1)S(1)}, bf16[1,64,4096]{2,1,0:T(8,128)(2,1)S(1)}, u32[]{:S(2)}, u32[]{:S(2)}) %collective-permute-start.1) | collective-permute-done | bytes 524320 | tf_op jit(solution)/shard_map/ppermute | solution.py:72
  66.6 0.9 bitcast_dynamic-update-slice_fusion.12
  67.4 12.8 %collective-permute-done.2 = bf16[1,64,4096]{2,1,0:T(8,128)(2,1)S(1)} collective-permute-done((bf16[1,64,4096]{2,1,0:T(8,128)(2,1)S(1)}, bf16[1,64,4096]{2,1,0:T(8,128)(2,1)S(1)}, u32[]{:S(2)}, u32[]{:S(2)}) %collective-permute-start.2) | collective-permute-done | bytes 524320 | tf_op jit(solution)/shard_map/ppermute | solution.py:72
  80.2 0.8 bitcast_dynamic-update-slice_fusion.11
  81.1 0.8 bitcast_dynamic-update-slice_fusion.10
  81.9 0.8 bitcast_dynamic-update-slice_fusion.9
  82.8 0.8 bitcast_dynamic-update-slice_fusion.8
  83.6 0.8 bitcast_dynamic-update-slice_fusion.7
  84.4 5.0 %gather_fusion = bf16[8,64,4096]{2,1,0:T(8,128)(2,1)} fusion(bf16[8,64,4096]{2,1,0:T(8,128)(2,1)} %bitcast.20, s32[1024]{0:T(1024)S(1)} %pad_clamp_fusion), kind=kCustom, calls=%fused_computation | custom fusion | bytes 8388640 | tf_op jit(solution)/shard_map/gather | solution.py:79
  89.4 2.7 copy.30
  92.1 2.0 copy-done
  94.1 3.4 fusion.10
  97.5 8.8 %fusion = bf16[4096,2,256]{0,2,1:T(8,128)(2,1)} fusion(bf16[2,2,192,4096]{3,2,1,0:T(8,128)(2,1)} %param.12, bf16[2,256,4096]{2,1,0:T(8,128)(2,1)} %bitcast.185, bf16[2,2,4096,192]{2,3,1,0:T(8,128)(2,1)} %param.11, f32[2,256,192]{1,2,0:T(8,128)S(1)} %fusion.10), kind=kOutput, calls=%fused_computation.6 | convolution fusion | flops 1613299712 | bytes 15073280 | tf_op jit(solution)/shard_map/erf,efd->der/dot_general | solution.py:96
  107.8 75.7 %reduce-scatter.3.cloned.1.call-done = bf16[1024,2,256]{0,2,1:T(8,128)(2,1)} async-done(((bf16[4096,2,256]{0,2,1:T(8,128)(2,1)}), bf16[1024,2,256]{0,2,1:T(8,128)(2,1)}) %reduce-scatter.3.cloned.1.call-update) | async-done | bytes 1048592 | tf_op jit(solution)/shard_map/reduce_scatter | solution.py:98
  183.5 2.3 copy.31
  185.8 3.7 all-to-all-start
  190.2 14.7 %all-to-all-done = bf16[8,64,1024]{2,1,0:T(8,128)(2,1)S(1)} async-done(((bf16[8,64,1024]{2,1,0:T(8,128)(2,1)}), bf16[8,64,1024]{2,1,0:T(8,128)(2,1)S(1)}, u32[]{:S(2)}, u32[]{:S(2)}) %all-to-all-start) | async-done | bytes 1048608 | tf_op jit(solution)/shard_map/all_to_all | solution.py:103
  205.5 14.5 %all_gather.7 = bf16[32,4096]{1,0:T(8,128)(2,1)S(1)} all-gather(bf16[32,1024]{1,0:T(8,128)(2,1)S(1)} %fusion.30), channel_id=1, replica_groups=mesh['ep'=8,'tp'=4] {'tp'}, dimensions={1}, use_global_device_ids=true | all-gather | bytes 327680 | tf_op jit(solution)/shard_map/all_gather | solution.py:39
  220.2 1.3 convolution_convert_fusion.1
  221.5 1.3 dynamic-slice_bitcast_fusion
  223.5 2.3 collective-permute-start.12
  226.3 0.9 collective-permute-start.10
  227.8 0.8 bitcast_dynamic-update-slice_fusion.6
  228.7 31.4 %collective-permute-done.8 = bf16[1,64,4096]{2,1,0:T(8,128)(2,1)S(1)} collective-permute-done((bf16[1,64,4096]{2,1,0:T(8,128)(2,1)S(1)}, bf16[1,64,4096]{2,1,0:T(8,128)(2,1)S(1)}, u32[]{:S(2)}, u32[]{:S(2)}) %collective-permute-start.8) | collective-permute-done | bytes 524320 | tf_op jit(solution)/shard_map/ppermute | solution.py:72
  260.1 0.9 bitcast_dynamic-update-slice_fusion.5
  261.0 13.0 %collective-permute-done.9 = bf16[1,64,4096]{2,1,0:T(8,128)(2,1)S(1)} collective-permute-done((bf16[1,64,4096]{2,1,0:T(8,128)(2,1)S(1)}, bf16[1,64,4096]{2,1,0:T(8,128)(2,1)S(1)}, u32[]{:S(2)}, u32[]{:S(2)}) %collective-permute-start.9) | collective-permute-done | bytes 524320 | tf_op jit(solution)/shard_map/ppermute | solution.py:72
  273.9 0.8 bitcast_dynamic-update-slice_fusion.4
  274.8 0.8 bitcast_dynamic-update-slice_fusion.3
  275.6 0.8 bitcast_dynamic-update-slice_fusion.2
  277.3 0.8 bitcast_dynamic-update-slice_fusion
  278.2 5.0 %gather_fusion.1 = bf16[8,64,4096]{2,1,0:T(8,128)(2,1)} fusion(bf16[8,64,4096]{2,1,0:T(8,128)(2,1)} %bitcast.54, s32[1024]{0:T(1024)S(1)} %pad_clamp_fusion), kind=kCustom, calls=%fused_computation.1 | custom fusion | bytes 8388640 | tf_op jit(solution)/shard_map/gather | solution.py:79
  283.1 2.7 copy.36
  285.8 2.0 copy-done.1
  287.8 3.4 fusion.5
  291.2 8.8 %fusion.1 = bf16[4096,2,256]{0,2,1:T(8,128)(2,1)} fusion(bf16[2,2,192,4096]{3,2,1,0:T(8,128)(2,1)} %param.12, bf16[2,256,4096]{2,1,0:T(8,128)(2,1)} %bitcast.187, bf16[2,2,4096,192]{2,3,1,0:T(8,128)(2,1)} %param.11, f32[2,256,192]{1,2,0:T(8,128)S(1)} %fusion.5), kind=kOutput, calls=%fused_computation.7 | convolution fusion | flops 1613299712 | bytes 15073280 | tf_op jit(solution)/shard_map/erf,efd->der/dot_general | solution.py:96
  300.0 75.8 %reduce-scatter.5.cloned.1.call-done = bf16[1024,2,256]{0,2,1:T(8,128)(2,1)} async-done(((bf16[4096,2,256]{0,2,1:T(8,128)(2,1)}), bf16[1024,2,256]{0,2,1:T(8,128)(2,1)}) %reduce-scatter.5.cloned.1.call-update) | async-done | bytes 1048592 | tf_op jit(solution)/shard_map/reduce_scatter | solution.py:98
  375.8 2.3 copy.37
  378.1 3.6 all-to-all-start.1
  382.4 14.8 %all-to-all-done.1 = bf16[8,64,1024]{2,1,0:T(8,128)(2,1)S(1)} async-done(((bf16[8,64,1024]{2,1,0:T(8,128)(2,1)}), bf16[8,64,1024]{2,1,0:T(8,128)(2,1)S(1)}, u32[]{:S(2)}, u32[]{:S(2)}) %all-to-all-start.1) | async-done | bytes 1048608 | tf_op jit(solution)/shard_map/all_to_all | solution.py:103
  397.1 1.2 fusion.31
  (76 shorter events, 10.2 us)
Async XLA Ops:
  6.5 177.0 %reduce-scatter.3.cloned.1.call-start = ((), (), s32[]{:S(2)}) async-start(), calls=%async_computation.4 | async-start | bytes 5242880 | tf_op jit(solution)/shard_map/reduce_scatter | solution.py:98
  28.3 4.6 %collective-permute-start = (bf16[1,64,4096]{2,1,0:T(8,128)(2,1)S(1)}, bf16[1,64,4096]{2,1,0:T(8,128)(2,1)S(1)}, u32[]{:S(2)}, u32[]{:S(2)}) collective-permute-start(bf16[1,64,4096]{2,1,0:T(8,128)(2,1)S(1)} %get-tuple-element.19), channel_id=1, source_target_pairs={{0,4},{4,0},{8,12},{12,8},{16,20},{20,16},{24,28},{28,24},{1,5},{5... | collective-permute-start | bytes 1572872 | tf_op jit(solution)/shard_map/ppermute | solution.py:72
  28.3 55.2 %collective-permute-start.6 = (bf16[1,64,4096]{2,1,0:T(8,128)(2,1)S(1)}, bf16[1,64,4096]{2,1,0:T(8,128)(2,1)S(1)}, u32[]{:S(2)}, u32[]{:S(2)}) collective-permute-start(bf16[1,64,4096]{2,1,0:T(8,128)(2,1)S(1)} %get-tuple-element.13), channel_id=1, source_target_pairs={{0,28},{4,24},{8,20},{12,16},{16,12},{20,8},{24,4},{28,0},{1,29},{... | collective-permute-start | bytes 1572872 | tf_op jit(solution)/shard_map/ppermute | solution.py:72
  30.9 51.9 %collective-permute-start.5 = (bf16[1,64,4096]{2,1,0:T(8,128)(2,1)S(1)}, bf16[1,64,4096]{2,1,0:T(8,128)(2,1)S(1)}, u32[]{:S(2)}, u32[]{:S(2)}) collective-permute-start(bf16[1,64,4096]{2,1,0:T(8,128)(2,1)S(1)} %get-tuple-element.14), channel_id=1, source_target_pairs={{0,24},{4,28},{8,16},{12,20},{16,8},{20,12},{24,0},{28,4},{1,25},{... | collective-permute-start | bytes 1572872 | tf_op jit(solution)/shard_map/ppermute | solution.py:72
  31.4 50.5 %collective-permute-start.4 = (bf16[1,64,4096]{2,1,0:T(8,128)(2,1)S(1)}, bf16[1,64,4096]{2,1,0:T(8,128)(2,1)S(1)}, u32[]{:S(2)}, u32[]{:S(2)}) collective-permute-start(bf16[1,64,4096]{2,1,0:T(8,128)(2,1)S(1)} %get-tuple-element.15), channel_id=1, source_target_pairs={{0,20},{4,16},{8,28},{12,24},{16,4},{20,0},{24,12},{28,8},{1,21},{... | collective-permute-start | bytes 1572872 | tf_op jit(solution)/shard_map/ppermute | solution.py:72
  32.2 48.8 %collective-permute-start.3 = (bf16[1,64,4096]{2,1,0:T(8,128)(2,1)S(1)}, bf16[1,64,4096]{2,1,0:T(8,128)(2,1)S(1)}, u32[]{:S(2)}, u32[]{:S(2)}) collective-permute-start(bf16[1,64,4096]{2,1,0:T(8,128)(2,1)S(1)} %get-tuple-element.16), channel_id=1, source_target_pairs={{0,16},{4,20},{8,24},{12,28},{16,0},{20,4},{24,8},{28,12},{1,17},{... | collective-permute-start | bytes 1572872 | tf_op jit(solution)/shard_map/ppermute | solution.py:72
  32.9 33.1 %collective-permute-start.1 = (bf16[1,64,4096]{2,1,0:T(8,128)(2,1)S(1)}, bf16[1,64,4096]{2,1,0:T(8,128)(2,1)S(1)}, u32[]{:S(2)}, u32[]{:S(2)}) collective-permute-start(bf16[1,64,4096]{2,1,0:T(8,128)(2,1)S(1)} %get-tuple-element.18), channel_id=1, source_target_pairs={{0,8},{4,12},{8,0},{12,4},{16,24},{20,28},{24,16},{28,20},{1,9},{5... | collective-permute-start | bytes 1572872 | tf_op jit(solution)/shard_map/ppermute | solution.py:72
  66.0 14.2 %collective-permute-start.2 = (bf16[1,64,4096]{2,1,0:T(8,128)(2,1)S(1)}, bf16[1,64,4096]{2,1,0:T(8,128)(2,1)S(1)}, u32[]{:S(2)}, u32[]{:S(2)}) collective-permute-start(bf16[1,64,4096]{2,1,0:T(8,128)(2,1)S(1)} %get-tuple-element.17), channel_id=1, source_target_pairs={{0,12},{4,8},{8,4},{12,0},{16,28},{20,24},{24,20},{28,16},{1,13},{... | collective-permute-start | bytes 1572872 | tf_op jit(solution)/shard_map/ppermute | solution.py:72
  92.1 2.0 copy-start
  106.3 1.3 copy-start.3
  106.3 98.6 %copy-start.2 = (bf16[32,1024]{1,0:T(8,128)(2,1)S(1)}, bf16[32,1024]{1,0:T(8,128)(2,1)}, u32[]{:S(2)}) copy-start(bf16[32,1024]{1,0:T(8,128)(2,1)} %param.7) | copy-start | bytes 196612
  185.8 19.0 %all-to-all-start = ((bf16[8,64,1024]{2,1,0:T(8,128)(2,1)}), bf16[8,64,1024]{2,1,0:T(8,128)(2,1)S(1)}, u32[]{:S(2)}, u32[]{:S(2)}) async-start(bf16[8,64,1024]{2,1,0:T(8,128)(2,1)} %bitcast.32), calls=%async_computation.1 | async-start | bytes 2097152 | tf_op jit(solution)/shard_map/all_to_all | solution.py:103
  189.5 186.3 %reduce-scatter.5.cloned.1.call-start = ((), (), s32[]{:S(2)}) async-start(), calls=%async_computation.5 | async-start | bytes 5242880 | tf_op jit(solution)/shard_map/reduce_scatter | solution.py:98
  222.8 4.4 %collective-permute-start.7 = (bf16[1,64,4096]{2,1,0:T(8,128)(2,1)S(1)}, bf16[1,64,4096]{2,1,0:T(8,128)(2,1)S(1)}, u32[]{:S(2)}, u32[]{:S(2)}) collective-permute-start(bf16[1,64,4096]{2,1,0:T(8,128)(2,1)S(1)} %get-tuple-element.11), channel_id=1, source_target_pairs={{0,4},{4,0},{8,12},{12,8},{16,20},{20,16},{24,28},{28,24},{1,5},{5... | collective-permute-start | bytes 1572872 | tf_op jit(solution)/shard_map/ppermute | solution.py:72
  222.8 54.5 %collective-permute-start.13 = (bf16[1,64,4096]{2,1,0:T(8,128)(2,1)S(1)}, bf16[1,64,4096]{2,1,0:T(8,128)(2,1)S(1)}, u32[]{:S(2)}, u32[]{:S(2)}) collective-permute-start(bf16[1,64,4096]{2,1,0:T(8,128)(2,1)S(1)} %get-tuple-element.5), channel_id=1, source_target_pairs={{0,28},{4,24},{8,20},{12,16},{16,12},{20,8},{24,4},{28,0},{1,29},{... | collective-permute-start | bytes 1572872 | tf_op jit(solution)/shard_map/ppermute | solution.py:72
  223.5 53.0 %collective-permute-start.12 = (bf16[1,64,4096]{2,1,0:T(8,128)(2,1)S(1)}, bf16[1,64,4096]{2,1,0:T(8,128)(2,1)S(1)}, u32[]{:S(2)}, u32[]{:S(2)}) collective-permute-start(bf16[1,64,4096]{2,1,0:T(8,128)(2,1)S(1)} %get-tuple-element.6), channel_id=1, source_target_pairs={{0,24},{4,28},{8,16},{12,20},{16,8},{20,12},{24,0},{28,4},{1,25},{... | collective-permute-start | bytes 1572872 | tf_op jit(solution)/shard_map/ppermute | solution.py:72
  225.8 49.8 %collective-permute-start.11 = (bf16[1,64,4096]{2,1,0:T(8,128)(2,1)S(1)}, bf16[1,64,4096]{2,1,0:T(8,128)(2,1)S(1)}, u32[]{:S(2)}, u32[]{:S(2)}) collective-permute-start(bf16[1,64,4096]{2,1,0:T(8,128)(2,1)S(1)} %get-tuple-element.7), channel_id=1, source_target_pairs={{0,20},{4,16},{8,28},{12,24},{16,4},{20,0},{24,12},{28,8},{1,21},{... | collective-permute-start | bytes 1572872 | tf_op jit(solution)/shard_map/ppermute | solution.py:72
  226.3 48.5 %collective-permute-start.10 = (bf16[1,64,4096]{2,1,0:T(8,128)(2,1)S(1)}, bf16[1,64,4096]{2,1,0:T(8,128)(2,1)S(1)}, u32[]{:S(2)}, u32[]{:S(2)}) collective-permute-start(bf16[1,64,4096]{2,1,0:T(8,128)(2,1)S(1)} %get-tuple-element.8), channel_id=1, source_target_pairs={{0,16},{4,20},{8,24},{12,28},{16,0},{20,4},{24,8},{28,12},{1,17},{... | collective-permute-start | bytes 1572872 | tf_op jit(solution)/shard_map/ppermute | solution.py:72
  227.2 32.9 %collective-permute-start.8 = (bf16[1,64,4096]{2,1,0:T(8,128)(2,1)S(1)}, bf16[1,64,4096]{2,1,0:T(8,128)(2,1)S(1)}, u32[]{:S(2)}, u32[]{:S(2)}) collective-permute-start(bf16[1,64,4096]{2,1,0:T(8,128)(2,1)S(1)} %get-tuple-element.10), channel_id=1, source_target_pairs={{0,8},{4,12},{8,0},{12,4},{16,24},{20,28},{24,16},{28,20},{1,9},{5... | collective-permute-start | bytes 1572872 | tf_op jit(solution)/shard_map/ppermute | solution.py:72
  260.1 13.8 %collective-permute-start.9 = (bf16[1,64,4096]{2,1,0:T(8,128)(2,1)S(1)}, bf16[1,64,4096]{2,1,0:T(8,128)(2,1)S(1)}, u32[]{:S(2)}, u32[]{:S(2)}) collective-permute-start(bf16[1,64,4096]{2,1,0:T(8,128)(2,1)S(1)} %get-tuple-element.9), channel_id=1, source_target_pairs={{0,12},{4,8},{8,4},{12,0},{16,28},{20,24},{24,20},{28,16},{1,13},{... | collective-permute-start | bytes 1572872 | tf_op jit(solution)/shard_map/ppermute | solution.py:72
  285.8 2.0 copy-start.1
  378.1 19.0 %all-to-all-start.1 = ((bf16[8,64,1024]{2,1,0:T(8,128)(2,1)}), bf16[8,64,1024]{2,1,0:T(8,128)(2,1)S(1)}, u32[]{:S(2)}, u32[]{:S(2)}) async-start(bf16[8,64,1024]{2,1,0:T(8,128)(2,1)} %bitcast.65), calls=%async_computation.3 | async-start | bytes 2097152 | tf_op jit(solution)/shard_map/all_to_all | solution.py:103
Sparse Core Ops, SparseCore 0:
  106.4 77.0 reduce-scatter.2
  300.2 75.6 reduce-scatter.4
